TPU v7x, 128 devices: a whole 4x4x4 slice. The times are simulated.
128 devices in a mesh: rows: 4 (over x), cols: 8 (over z, core), slabs: 4 (over y).
Axes of the slice: x: 4, y: 4, z: 4, core: 2. Of those that a mesh axis runs over, the one named last changes fastest.
Arguments:
- field_values: float32 [16, 256, 512, 128], P('rows', 'cols', 'slabs'), may hold values from 0.5 to 2
- mobility: float32 [16, 256, 512, 128], P('rows', 'cols', 'slabs'), may hold values from 0.03 to 0.15
- source: float32 [16, 256, 512, 128], P('rows', 'cols', 'slabs'), may hold values from -0.2 to 0.2
Outputs:
- anomaly: float32 [16, 256, 512, 128], P('rows', 'cols', 'slabs')
- field_values_end: float32 [16, 256, 512, 128], P('rows', 'cols', 'slabs')
All inputs are finite; a program needn't handle non-finite values.
Results may differ from a plain program's by a relative error of at most 0.00002.
Values sent between devices are 32-bit elements; how exact they have to be, the bound alone decides.
A program may use at most 128 MiB of HBM per device.

v0:
```python
import jax
import jax.numpy as jnp
from jax import lax
from jax.sharding import PartitionSpec as P

STEPS = 3


def padded_2(shard, sides, width):
    edges = {}
    for axis, dim in sides:
        size, length = (lax.axis_size(axis), shard.shape[dim])
        up = [(i, (i + 1) % size) for i in range(size)]
        last = lax.slice_in_dim(shard, length - width, length, axis=dim)
        initial = lax.slice_in_dim(shard, 0, width, axis=dim)
        edges[dim] = (
            lax.ppermute(last, axis, up),
            lax.ppermute(initial, axis, [(b, a) for a, b in up]),
        )
    done = []
    for _, dim in sides:
        low, high = edges[dim]
        around = [(width, width) if d in done else (0, 0) for d in range(shard.ndim)]
        shard = jnp.concatenate([jnp.pad(low, around), shard, jnp.pad(high, around)], axis=dim)
        done.append(dim)
    return shard


def copy_for_each(shard, axis):
    copies = jnp.broadcast_to(shard, (lax.axis_size(axis), *shard.shape))
    return lax.all_to_all(copies, axis, split_axis=0, concat_axis=0, tiled=True)


def taken_together(shard, axis):
    everything = copy_for_each(shard, axis)
    return jnp.sum(everything, axis=0)


def in_one(arrays, axis):
    ends = [0]
    for a in arrays:
        ends.append(ends[-1] + a.size)
    subtotal = taken_together(jnp.concatenate([a.ravel() for a in arrays]), axis)
    return tuple((subtotal[b:e].reshape(a.shape) for a, b, e in zip(arrays, ends, ends[1:])))


def strip_edges(values, dims):
    for dim in dims:
        values = lax.slice_in_dim(values, 1, values.shape[dim] - 1, axis=dim)
    return values


def neighbour(values, dim, start, dims):
    others = [other for other in dims if other != dim]
    values = strip_edges(values, others)
    return lax.slice_in_dim(values, start, start + values.shape[dim] - 2, axis=dim)


def one_step(padded, mobility, source):
    middle = strip_edges(padded, (0, 1, 2))
    lower = [neighbour(padded, dim, 0, (0, 1, 2)) for dim in (0, 1, 2)]
    upper = [neighbour(padded, dim, 2, (0, 1, 2)) for dim in (0, 1, 2)]
    spread = lower[0] + upper[0] + lower[1] + upper[1] + lower[2] + upper[2] - 6.0 * middle
    return middle + mobility * spread + source


def per_device(field_values, mobility, source):
    for step in range(STEPS):
        padded = padded_2(field_values, (("rows", 0), ("cols", 1), ("slabs", 2)), 1)
        field_values = one_step(padded, mobility, source)
    count = field_values.shape[2] * lax.axis_size("slabs")
    guess = 1.0
    moved = field_values - guess
    totals, squares = in_one(
        (jnp.sum(moved, axis=2, keepdims=True), jnp.sum(moved * moved, axis=2, keepdims=True)),
        "slabs",
    )
    line_mean = guess + totals / count
    centred = field_values - line_mean
    line_variance = squares / count - totals / count * (totals / count)
    anomaly = centred * lax.rsqrt(line_variance + 0.0001)
    return (anomaly, field_values)


def solution(mesh):
    return jax.shard_map(
        per_device,
        mesh=mesh,
        in_specs=(
            P("rows", "cols", "slabs", None),
            P("rows", "cols", "slabs", None),
            P("rows", "cols", "slabs", None),
        ),
        out_specs=(P("rows", "cols", "slabs", None), P("rows", "cols", "slabs", None)),
        check_vma=False,
    )
```

profile of v0, /device:TPU:0, one launch (start us, length us, event | category | flops | bytes accessed | tf_op | source)
XLA Modules:
  0.0 267.1 jit_solution(17517863620219522099)
XLA Ops:
  0.6 0.0 copy-start
  0.6 4.1 %fusion.46 = (f32[1,32,128,128]{3,2,1,0:T(8,128)}, f32[1,32,128,128]{3,2,1,0:T(8,128)S(1)}) fusion(f32[4,32,128,128]{3,2,1,0:T(8,128)} %param.3), kind=kLoop, calls=%fused_computation.102 | loop fusion | bytes 8388608 | tf_op jit(solution)/shard_map/slice | solution.py:15
  4.7 1.6 collective-permute-start
  6.3 1.6 collective-permute-start.1
  8.0 0.0 collective-permute-start.2
  8.0 3.0 %collective-permute-start.3 = (f32[4,1,128,128]{3,2,1,0:T(8,128)S(1)}, f32[4,1,128,128]{3,2,1,0:T(8,128)S(1)}, u32[]{:S(2)}, u32[]{:S(2)}) collective-permute-start(f32[4,1,128,128]{3,2,1,0:T(8,128)S(1)} %get-tuple-element.20), channel_id=1, source_target_pairs={{4,0},{8,4},{12,8},{16,12},{20,16},{24,20},{28,24},{0,28},{5,1},{9... | collective-permute-start | bytes 786440 | tf_op jit(solution)/shard_map/ppermute | solution.py:18
  11.1 0.7 fusion.44
  11.8 1.6 collective-permute-start.4
  13.4 1.7 collective-permute-done.2
  15.1 3.0 %collective-permute-start.5 = (f32[4,32,1,128]{3,2,1,0:T(1,128)S(1)}, f32[4,32,1,128]{3,2,1,0:T(1,128)S(1)}, u32[]{:S(2)}, u32[]{:S(2)}) collective-permute-start(f32[4,32,1,128]{3,2,1,0:T(1,128)S(1)} %get-tuple-element.18), channel_id=1, source_target_pairs={{1,0},{2,1},{3,2},{0,3},{5,4},{6,5},{7,6},{4,7},{9,8},{10,9},{11,1... | collective-permute-start | bytes 196616 | tf_op jit(solution)/shard_map/ppermute | solution.py:18
  18.2 35.0 %collective-permute-done = f32[1,32,128,128]{3,2,1,0:T(8,128)S(1)} collective-permute-done((f32[1,32,128,128]{3,2,1,0:T(8,128)S(1)}, f32[1,32,128,128]{3,2,1,0:T(8,128)S(1)}, u32[]{:S(2)}, u32[]{:S(2)}) %collective-permute-start) | collective-permute-done | bytes 2097184 | tf_op jit(solution)/shard_map/ppermute | solution.py:17
  53.2 1.5 constant_dynamic-update-slice_fusion.2
  54.7 4.7 %constant_dynamic-update-slice_fusion.1 = f32[6,32,128,128]{3,2,1,0:T(8,128)} fusion(f32[6,32,128,128]{3,2,1,0:T(8,128)} %constant_dynamic-update-slice_fusion.2, f32[4,32,128,128]{3,2,1,0:T(8,128)S(1)} %copy-done), kind=kLoop, calls=%fused_computation.92 | loop fusion | bytes 16777216
  59.4 1.3 copy-done.1
  60.8 1.5 constant_dynamic-update-slice_fusion
  62.2 0.0 collective-permute-done.4
  62.2 0.0 collective-permute-done.5
  62.3 25.9 %fusion.27 = f32[4,32,128,128]{3,2,1,0:T(8,128)} fusion(f32[4,32,128,128]{3,2,1,0:T(8,128)S(1)} %bitcast.5, f32[4,32,128,128]{3,2,1,0:T(8,128)} %param.3, f32[4,32,128,128]{3,2,1,0:T(8,128)} %param.4, f32[4,32,1,128]{3,2,1,0:T(1,128)S(1)} %collective-permute-done.5, f32[6,1,128,128]{3,2,1,0:T(8,128)S(1)} %pad.39, ...), kind=kLoop, calls=%fused_computation.64 | loop fusion | flops 54525952 | bytes 51249152 | tf_op jit(solution)/shard_map/add | solution.py:64
  88.2 2.5 fusion.42
  90.7 0.5 collective-permute-start.6
  91.2 2.8 %collective-permute-start.7 = (f32[1,32,128,128]{3,2,1,0:T(8,128)S(1)}, f32[1,32,128,128]{3,2,1,0:T(8,128)}, u32[]{:S(2)}, u32[]{:S(2)}) collective-permute-start(f32[1,32,128,128]{3,2,1,0:T(8,128)S(1)} %get-tuple-element.14), channel_id=1, source_target_pairs={{32,0},{64,32},{96,64},{0,96},{33,1},{65,33},{97,65},{1,97},{34,2}... | collective-permute-start | bytes 6291464 | tf_op jit(solution)/shard_map/ppermute | solution.py:18
  94.0 1.1 fusion.43
  95.1 0.0 collective-permute-start.8
  95.1 2.9 %collective-permute-start.9 = (f32[4,1,128,128]{3,2,1,0:T(8,128)S(1)}, f32[4,1,128,128]{3,2,1,0:T(8,128)S(1)}, u32[]{:S(2)}, u32[]{:S(2)}) collective-permute-start(f32[4,1,128,128]{3,2,1,0:T(8,128)S(1)} %get-tuple-element.16), channel_id=1, source_target_pairs={{4,0},{8,4},{12,8},{16,12},{20,16},{24,20},{28,24},{0,28},{5,1},{9... | collective-permute-start | bytes 786440 | tf_op jit(solution)/shard_map/ppermute | solution.py:18
  98.0 1.3 fusion.41
  99.3 1.8 collective-permute-start.10
  101.2 0.9 collective-permute-done.8
  102.1 3.2 %collective-permute-start.11 = (f32[4,32,1,128]{3,2,1,0:T(1,128)S(1)}, f32[4,32,1,128]{3,2,1,0:T(1,128)S(1)}, u32[]{:S(2)}, u32[]{:S(2)}) collective-permute-start(f32[4,32,1,128]{3,2,1,0:T(1,128)S(1)} %get-tuple-element.12), channel_id=1, source_target_pairs={{1,0},{2,1},{3,2},{0,3},{5,4},{6,5},{7,6},{4,7},{9,8},{10,9},{11,1... | collective-permute-start | bytes 196616 | tf_op jit(solution)/shard_map/ppermute | solution.py:18
  105.4 1.8 collective-permute-done.11
  107.2 31.2 %collective-permute-done.6 = f32[1,32,128,128]{3,2,1,0:T(8,128)S(1)} collective-permute-done((f32[1,32,128,128]{3,2,1,0:T(8,128)S(1)}, f32[1,32,128,128]{3,2,1,0:T(8,128)S(1)}, u32[]{:S(2)}, u32[]{:S(2)}) %collective-permute-start.6) | collective-permute-done | bytes 2097184 | tf_op jit(solution)/shard_map/ppermute | solution.py:17
  138.4 28.2 %fusion.16 = f32[4,32,128,128]{3,2,1,0:T(8,128)} fusion(f32[4,32,128,128]{3,2,1,0:T(8,128)} %param.5, f32[4,32,128,128]{3,2,1,0:T(8,128)} %fusion.27, f32[4,32,128,128]{3,2,1,0:T(8,128)} %param.4, f32[4,32,1,128]{3,2,1,0:T(1,128)S(1)} %collective-permute-done.11, f32[6,1,128,128]{3,2,1,0:T(8,128)S(1)} %pad.43, f32[6,1,128,128]{3,2,1,0:T(8,128)S(1)} %pad.42, ...), kind=kLoop, calls=%fused_computation.35 | loop fusion | flops 71303168 | bytes 38666240 | tf_op jit(solution)/shard_map/add | solution.py:64
  166.6 2.5 fusion.40
  169.1 0.7 collective-permute-start.12
  169.9 2.7 collective-permute-start.13
  172.5 1.1 fusion.39
  173.6 0.0 collective-permute-start.14
  173.6 2.9 %collective-permute-start.15 = (f32[4,1,128,128]{3,2,1,0:T(8,128)S(1)}, f32[4,1,128,128]{3,2,1,0:T(8,128)S(1)}, u32[]{:S(2)}, u32[]{:S(2)}) collective-permute-start(f32[4,1,128,128]{3,2,1,0:T(8,128)S(1)} %get-tuple-element.8), channel_id=1, source_target_pairs={{4,0},{8,4},{12,8},{16,12},{20,16},{24,20},{28,24},{0,28},{5,1},{9... | collective-permute-start | bytes 786440 | tf_op jit(solution)/shard_map/ppermute | solution.py:18
  176.6 1.3 fusion.38
  177.9 1.9 collective-permute-start.16
  179.8 0.8 collective-permute-done.14
  180.6 3.3 %collective-permute-start.17 = (f32[4,32,1,128]{3,2,1,0:T(1,128)S(1)}, f32[4,32,1,128]{3,2,1,0:T(1,128)S(1)}, u32[]{:S(2)}, u32[]{:S(2)}) collective-permute-start(f32[4,32,1,128]{3,2,1,0:T(1,128)S(1)} %get-tuple-element.6), channel_id=1, source_target_pairs={{1,0},{2,1},{3,2},{0,3},{5,4},{6,5},{7,6},{4,7},{9,8},{10,9},{11,1... | collective-permute-start | bytes 196616 | tf_op jit(solution)/shard_map/ppermute | solution.py:18
  184.0 1.8 collective-permute-done.17
  185.8 30.2 %collective-permute-done.12 = f32[1,32,128,128]{3,2,1,0:T(8,128)S(1)} collective-permute-done((f32[1,32,128,128]{3,2,1,0:T(8,128)S(1)}, f32[1,32,128,128]{3,2,1,0:T(8,128)S(1)}, u32[]{:S(2)}, u32[]{:S(2)}) %collective-permute-start.12) | collective-permute-done | bytes 2097184 | tf_op jit(solution)/shard_map/ppermute | solution.py:17
  216.0 28.7 %add_reduce_fusion = (f32[4,32,128]{2,1,0:T(8,128)S(1)}, f32[4,32,128]{2,1,0:T(8,128)S(1)}, f32[4,32,128,128]{3,2,1,0:T(8,128)}) fusion(f32[4,32,128,128]{3,2,1,0:T(8,128)} %param.5, f32[4,32,128,128]{3,2,1,0:T(8,128)} %fusion.16, f32[4,32,128,128]{3,2,1,0:T(8,128)} %param.4, f32[4,32,1,128]{3,2,1,0:T(1,128)S(1)} %collective-permute-done.17, ...), kind=kLoop, calls=%fused_computation.83 | loop fusion | flops 79659008 | bytes 38797312 | tf_op jit(solution)/shard_map/reduce_sum | solution.py:75
  244.7 0.3 broadcast_in_dim.3
  245.0 12.7 %all_to_all.6 = f32[4,1,32768]{2,1,0:T(1,128)S(1)} all-to-all(f32[4,1,32768]{2,1,0:T(1,128)S(1)} %broadcast_in_dim.3), channel_id=1, replica_groups=mesh['rows'=4,'cols'=8,'slabs'=4] {'slabs'}, dimensions={0} | all-to-all | bytes 1048576 | tf_op jit(solution)/shard_map/all_to_all | solution.py:31
  257.7 0.5 reduce_sum.29
  258.2 8.8 %subtract_multiply_fusion = f32[4,32,128,128]{3,2,1,0:T(8,128)} fusion(f32[4,32,128,128]{3,2,1,0:T(8,128)} %get-tuple-element.4, f32[4,32,128]{2,1,0:T(8,128)S(1)} %bitcast.9, f32[4,32,128]{2,1,0:T(8,128)S(1)} %bitcast.8), kind=kLoop, calls=%fused_computation.81 | loop fusion | flops 4194304 | bytes 16908288 | tf_op jit(solution)/shard_map/mul | solution.py:81
  (24 shorter events, 0.3 us)
Async XLA Ops:
  0.6 7.3 %copy-start = (f32[4,32,128,128]{3,2,1,0:T(8,128)S(1)}, f32[4,32,128,128]{3,2,1,0:T(8,128)}, u32[]{:S(2)}) copy-start(f32[4,32,128,128]{3,2,1,0:T(8,128)} %param.3) | copy-start | bytes 25165828
  4.7 48.5 %collective-permute-start = (f32[1,32,128,128]{3,2,1,0:T(8,128)S(1)}, f32[1,32,128,128]{3,2,1,0:T(8,128)S(1)}, u32[]{:S(2)}, u32[]{:S(2)}) collective-permute-start(f32[1,32,128,128]{3,2,1,0:T(8,128)S(1)} %get-tuple-element.22), channel_id=1, source_target_pairs={{0,32},{32,64},{64,96},{96,0},{1,33},{33,65},{65,97},{97,1},{2,34}... | collective-permute-start | bytes 6291464 | tf_op jit(solution)/shard_map/ppermute | solution.py:17
  6.3 53.1 %collective-permute-start.1 = (f32[1,32,128,128]{3,2,1,0:T(8,128)}, f32[1,32,128,128]{3,2,1,0:T(8,128)S(1)}, u32[]{:S(2)}, u32[]{:S(2)}) collective-permute-start(f32[1,32,128,128]{3,2,1,0:T(8,128)} %get-tuple-element.21), channel_id=1, source_target_pairs={{32,0},{64,32},{96,64},{0,96},{33,1},{65,33},{97,65},{1,97},{34,2}... | collective-permute-start | bytes 6291464 | tf_op jit(solution)/shard_map/ppermute | solution.py:18
  8.0 7.1 %collective-permute-start.2 = (f32[4,1,128,128]{3,2,1,0:T(8,128)S(1)}, f32[4,1,128,128]{3,2,1,0:T(8,128)S(1)}, u32[]{:S(2)}, u32[]{:S(2)}) collective-permute-start(f32[4,1,128,128]{3,2,1,0:T(8,128)S(1)} %get-tuple-element.19), channel_id=1, source_target_pairs={{0,4},{4,8},{8,12},{12,16},{16,20},{20,24},{24,28},{28,0},{1,5},{5... | collective-permute-start | bytes 786440 | tf_op jit(solution)/shard_map/ppermute | solution.py:17
  8.0 10.2 %collective-permute-start.3 = (f32[4,1,128,128]{3,2,1,0:T(8,128)S(1)}, f32[4,1,128,128]{3,2,1,0:T(8,128)S(1)}, u32[]{:S(2)}, u32[]{:S(2)}) collective-permute-start(f32[4,1,128,128]{3,2,1,0:T(8,128)S(1)} %get-tuple-element.20), channel_id=1, source_target_pairs={{4,0},{8,4},{12,8},{16,12},{20,16},{24,20},{28,24},{0,28},{5,1},{9... | collective-permute-start | bytes 786440 | tf_op jit(solution)/shard_map/ppermute | solution.py:18
  11.8 50.5 %collective-permute-start.4 = (f32[4,32,1,128]{3,2,1,0:T(1,128)}, f32[4,32,1,128]{3,2,1,0:T(1,128)S(1)}, u32[]{:S(2)}, u32[]{:S(2)}) collective-permute-start(f32[4,32,1,128]{3,2,1,0:T(1,128)} %get-tuple-element.17), channel_id=1, source_target_pairs={{0,1},{1,2},{2,3},{3,0},{4,5},{5,6},{6,7},{7,4},{8,9},{9,10},{10,1... | collective-permute-start | bytes 196616 | tf_op jit(solution)/shard_map/ppermute | solution.py:17
  15.1 47.2 %collective-permute-start.5 = (f32[4,32,1,128]{3,2,1,0:T(1,128)S(1)}, f32[4,32,1,128]{3,2,1,0:T(1,128)S(1)}, u32[]{:S(2)}, u32[]{:S(2)}) collective-permute-start(f32[4,32,1,128]{3,2,1,0:T(1,128)S(1)} %get-tuple-element.18), channel_id=1, source_target_pairs={{1,0},{2,1},{3,2},{0,3},{5,4},{6,5},{7,6},{4,7},{9,8},{10,9},{11,1... | collective-permute-start | bytes 196616 | tf_op jit(solution)/shard_map/ppermute | solution.py:18
  53.2 9.0 %slice-start = ((s8[8388608]{0:T(1024)(128)(4,1)}), s8[4194304]{0:T(1024)(128)(4,1)S(1)}, s32[]{:S(2)}) async-start(s8[8388608]{0:T(1024)(128)(4,1)} %bitcast.4), calls=%async_computation.1 | async-start | bytes 8388608
  54.7 7.6 %slice-start.1 = ((s8[8388608]{0:T(1024)(128)(4,1)}), s8[4194304]{0:T(1024)(128)(4,1)S(1)}, s32[]{:S(2)}) async-start(s8[8388608]{0:T(1024)(128)(4,1)} %bitcast.4), calls=%async_computation.2 | async-start | bytes 8388608
  59.4 1.3 copy-start.1
  90.7 47.7 %collective-permute-start.6 = (f32[1,32,128,128]{3,2,1,0:T(8,128)S(1)}, f32[1,32,128,128]{3,2,1,0:T(8,128)S(1)}, u32[]{:S(2)}, u32[]{:S(2)}) collective-permute-start(f32[1,32,128,128]{3,2,1,0:T(8,128)S(1)} %get-tuple-element.13), channel_id=1, source_target_pairs={{0,32},{32,64},{64,96},{96,0},{1,33},{33,65},{65,97},{97,1},{2,34}... | collective-permute-start | bytes 6291464 | tf_op jit(solution)/shard_map/ppermute | solution.py:17
  91.2 47.2 %collective-permute-start.7 = (f32[1,32,128,128]{3,2,1,0:T(8,128)S(1)}, f32[1,32,128,128]{3,2,1,0:T(8,128)}, u32[]{:S(2)}, u32[]{:S(2)}) collective-permute-start(f32[1,32,128,128]{3,2,1,0:T(8,128)S(1)} %get-tuple-element.14), channel_id=1, source_target_pairs={{32,0},{64,32},{96,64},{0,96},{33,1},{65,33},{97,65},{1,97},{34,2}... | collective-permute-start | bytes 6291464 | tf_op jit(solution)/shard_map/ppermute | solution.py:18
  95.1 7.0 %collective-permute-start.8 = (f32[4,1,128,128]{3,2,1,0:T(8,128)S(1)}, f32[4,1,128,128]{3,2,1,0:T(8,128)S(1)}, u32[]{:S(2)}, u32[]{:S(2)}) collective-permute-start(f32[4,1,128,128]{3,2,1,0:T(8,128)S(1)} %get-tuple-element.15), channel_id=1, source_target_pairs={{0,4},{4,8},{8,12},{12,16},{16,20},{20,24},{24,28},{28,0},{1,5},{5... | collective-permute-start | bytes 786440 | tf_op jit(solution)/shard_map/ppermute | solution.py:17
  95.1 10.2 %collective-permute-start.9 = (f32[4,1,128,128]{3,2,1,0:T(8,128)S(1)}, f32[4,1,128,128]{3,2,1,0:T(8,128)S(1)}, u32[]{:S(2)}, u32[]{:S(2)}) collective-permute-start(f32[4,1,128,128]{3,2,1,0:T(8,128)S(1)} %get-tuple-element.16), channel_id=1, source_target_pairs={{4,0},{8,4},{12,8},{16,12},{20,16},{24,20},{28,24},{0,28},{5,1},{9... | collective-permute-start | bytes 786440 | tf_op jit(solution)/shard_map/ppermute | solution.py:18
  99.3 6.0 %collective-permute-start.10 = (f32[4,32,1,128]{3,2,1,0:T(1,128)S(1)}, f32[4,32,1,128]{3,2,1,0:T(1,128)S(1)}, u32[]{:S(2)}, u32[]{:S(2)}) collective-permute-start(f32[4,32,1,128]{3,2,1,0:T(1,128)S(1)} %get-tuple-element.11), channel_id=1, source_target_pairs={{0,1},{1,2},{2,3},{3,0},{4,5},{5,6},{6,7},{7,4},{8,9},{9,10},{10,1... | collective-permute-start | bytes 196616 | tf_op jit(solution)/shard_map/ppermute | solution.py:17
  102.1 5.1 %collective-permute-start.11 = (f32[4,32,1,128]{3,2,1,0:T(1,128)S(1)}, f32[4,32,1,128]{3,2,1,0:T(1,128)S(1)}, u32[]{:S(2)}, u32[]{:S(2)}) collective-permute-start(f32[4,32,1,128]{3,2,1,0:T(1,128)S(1)} %get-tuple-element.12), channel_id=1, source_target_pairs={{1,0},{2,1},{3,2},{0,3},{5,4},{6,5},{7,6},{4,7},{9,8},{10,9},{11,1... | collective-permute-start | bytes 196616 | tf_op jit(solution)/shard_map/ppermute | solution.py:18
  169.1 46.9 %collective-permute-start.12 = (f32[1,32,128,128]{3,2,1,0:T(8,128)S(1)}, f32[1,32,128,128]{3,2,1,0:T(8,128)S(1)}, u32[]{:S(2)}, u32[]{:S(2)}) collective-permute-start(f32[1,32,128,128]{3,2,1,0:T(8,128)S(1)} %get-tuple-element.9), channel_id=1, source_target_pairs={{0,32},{32,64},{64,96},{96,0},{1,33},{33,65},{65,97},{97,1},{2,34}... | collective-permute-start | bytes 6291464 | tf_op jit(solution)/shard_map/ppermute | solution.py:17
  169.9 46.1 %collective-permute-start.13 = (f32[1,32,128,128]{3,2,1,0:T(8,128)S(1)}, f32[1,32,128,128]{3,2,1,0:T(8,128)}, u32[]{:S(2)}, u32[]{:S(2)}) collective-permute-start(f32[1,32,128,128]{3,2,1,0:T(8,128)S(1)} %get-tuple-element.10), channel_id=1, source_target_pairs={{32,0},{64,32},{96,64},{0,96},{33,1},{65,33},{97,65},{1,97},{34,2}... | collective-permute-start | bytes 6291464 | tf_op jit(solution)/shard_map/ppermute | solution.py:18
  173.6 7.0 %collective-permute-start.14 = (f32[4,1,128,128]{3,2,1,0:T(8,128)S(1)}, f32[4,1,128,128]{3,2,1,0:T(8,128)S(1)}, u32[]{:S(2)}, u32[]{:S(2)}) collective-permute-start(f32[4,1,128,128]{3,2,1,0:T(8,128)S(1)} %get-tuple-element.7), channel_id=1, source_target_pairs={{0,4},{4,8},{8,12},{12,16},{16,20},{20,24},{24,28},{28,0},{1,5},{5... | collective-permute-start | bytes 786440 | tf_op jit(solution)/shard_map/ppermute | solution.py:17
  173.6 10.3 %collective-permute-start.15 = (f32[4,1,128,128]{3,2,1,0:T(8,128)S(1)}, f32[4,1,128,128]{3,2,1,0:T(8,128)S(1)}, u32[]{:S(2)}, u32[]{:S(2)}) collective-permute-start(f32[4,1,128,128]{3,2,1,0:T(8,128)S(1)} %get-tuple-element.8), channel_id=1, source_target_pairs={{4,0},{8,4},{12,8},{16,12},{20,16},{24,20},{28,24},{0,28},{5,1},{9... | collective-permute-start | bytes 786440 | tf_op jit(solution)/shard_map/ppermute | solution.py:18
  177.9 6.1 %collective-permute-start.16 = (f32[4,32,1,128]{3,2,1,0:T(1,128)S(1)}, f32[4,32,1,128]{3,2,1,0:T(1,128)S(1)}, u32[]{:S(2)}, u32[]{:S(2)}) collective-permute-start(f32[4,32,1,128]{3,2,1,0:T(1,128)S(1)} %get-tuple-element.5), channel_id=1, source_target_pairs={{0,1},{1,2},{2,3},{3,0},{4,5},{5,6},{6,7},{7,4},{8,9},{9,10},{10,1... | collective-permute-start | bytes 196616 | tf_op jit(solution)/shard_map/ppermute | solution.py:17
  180.6 5.2 %collective-permute-start.17 = (f32[4,32,1,128]{3,2,1,0:T(1,128)S(1)}, f32[4,32,1,128]{3,2,1,0:T(1,128)S(1)}, u32[]{:S(2)}, u32[]{:S(2)}) collective-permute-start(f32[4,32,1,128]{3,2,1,0:T(1,128)S(1)} %get-tuple-element.6), channel_id=1, source_target_pairs={{1,0},{2,1},{3,2},{0,3},{5,4},{6,5},{7,6},{4,7},{9,8},{10,9},{11,1... | collective-permute-start | bytes 196616 | tf_op jit(solution)/shard_map/ppermute | solution.py:18
where the time goes:
time: 268 us; the launch traced here: 267 us
  waiting for transfers between devices  103 us (38%)
  other arithmetic  92.2 us (34%)
  starting transfers between devices  33.8 us (13%)
  local copies, waits for them, and re-layouts  24 us (9%)
  blocking collectives  12.7 us (5%)
    ppermute x9, waiting for transfers between devices, padded_2(): lax.ppermute(last, axis, up)  99.8 us
    add x2, other arithmetic, one_step(): return middle + mobility * spread + source  54.2 us
    reduce_sum x1, other arithmetic, per_device(): jnp.sum(moved, axis=2, keepdims=True)  28.7 us
    ppermute x9, starting transfers between devices, padded_2(): lax.ppermute(initial, axis, [(b, a) for a, b in up])  25.5 us
    all_to_all x1, blocking collectives, copy_for_each(): return lax.all_to_all(copies, axis, split_axis=0, concat_axis=0, tiled=True)  12.7 us
    slice x8, local copies, waits for them, and re-layouts, padded_2(): last = lax.slice_in_dim(shard, length - width, length, axis=dim)  10.5 us
    mul x1, other arithmetic, per_device(): anomaly = centred * lax.rsqrt(line_variance + 0.0001)  8.85 us
    ppermute x9, starting transfers between devices, padded_2(): lax.ppermute(last, axis, up)  8.3 us
  transfers between devices with their start and end apart: 18, of which 8 were waited for; matrix products, arithmetic and copies ran while one was open for 5% of the time, Pallas kernels for 0%

commit v1 on v0

v1 whole, which is shorter than its diff:
```python
import functools

import jax
import jax.numpy as jnp
from jax import lax
from jax.experimental import pallas as pl
from jax.experimental.pallas import tpu as pltpu
from jax.sharding import PartitionSpec as P

STEPS = 3
LINES = 2
EPS = 1e-4
MESH = pl.DeviceIdType.MESH
DMA = pltpu.SemaphoreType.DMA


def ring(axis, by):
    size = lax.axis_size(axis)
    return {axis: lax.rem(lax.axis_index(axis) + by % size, size)}


def remote(src, dst, send, recv, to):
    return pltpu.make_async_remote_copy(
        src_ref=src, dst_ref=dst, send_sem=send, recv_sem=recv, device_id=to, device_id_type=MESH
    )


def steps_kernel(
    field, mobility, source, odd, stats,
    even, mob, src, z_low, z_high, z_out,
    y_send, y_recv, x_send, x_recv, z_send, z_recv, s_send, s_recv, local,
):
    ny, nx, nz, _ = field.shape
    pieces = nx // LINES
    slabs = lax.axis_size("slabs")
    peers = [ring("rows", 1), ring("rows", -1), ring("cols", 1), ring("cols", -1)]
    peers += [ring("slabs", d) for d in range(1, slabs)]

    loads = [
        pltpu.make_async_copy(field, even.at[pl.ds(1, ny), pl.ds(1, nx)], local.at[0]),
        pltpu.make_async_copy(mobility, mob, local.at[1]),
        pltpu.make_async_copy(source, src, local.at[2]),
    ]
    barrier = pltpu.get_barrier_semaphore()
    for peer in peers:
        pl.semaphore_signal(barrier, inc=1, device_id=peer, device_id_type=MESH)
    for load in loads:
        load.start()
    pl.semaphore_wait(barrier, len(peers))

    def y_copies(n, c):
        buf = odd if n % 2 else even
        lines = pl.ds(1 + c * LINES, LINES)
        if n:
            first, last = buf.at[1, lines], buf.at[ny, lines]
        else:
            first, last = field.at[0, pl.ds(c * LINES, LINES)], field.at[ny - 1, pl.ds(c * LINES, LINES)]
        return (
            remote(last, buf.at[0, lines], y_send.at[n, 0, c], y_recv.at[n, 0, c], ring("rows", 1)),
            remote(first, buf.at[ny + 1, lines], y_send.at[n, 1, c], y_recv.at[n, 1, c], ring("rows", -1)),
        )

    def x_copies(n):
        buf = odd if n % 2 else even
        planes = pl.ds(1, ny)
        if n:
            first, last = buf.at[planes, 1], buf.at[planes, nx]
        else:
            first, last = field.at[:, 0], field.at[:, nx - 1]
        return (
            remote(last, buf.at[planes, 0], x_send.at[n, 0], x_recv.at[n, 0], ring("cols", 1)),
            remote(first, buf.at[planes, nx + 1], x_send.at[n, 1], x_recv.at[n, 1], ring("cols", -1)),
        )

    def z_copies(n):
        return (
            remote(z_out.at[n, 0], z_low.at[n], z_send.at[n, 0], z_recv.at[n, 0], ring("slabs", 1)),
            remote(z_out.at[n, 1], z_high.at[n], z_send.at[n, 1], z_recv.at[n, 1], ring("slabs", -1)),
        )

    def stat_copies(c):
        return [
            remote(stats.at[0, c], stats.at[d, c], s_send.at[d - 1, c], s_recv.at[d - 1, c], ring("slabs", d))
            for d in range(1, slabs)
        ]

    def start(copies):
        for copy in copies:
            copy.start()

    def arrived(copies):
        for copy in copies:
            copy.wait_recv()

    def sent(copies):
        for copy in copies:
            copy.wait_send()

    def each(count, body):
        def step(i, carry):
            body(i)
            return carry

        lax.fori_loop(0, count, step, 0)

    start(x_copies(0))
    each(pieces, lambda c: start(y_copies(0, c)))
    loads[0].wait()

    def pack(i):
        for y in range(ny):
            z_out[0, 0, y, pl.ds(i, 1)] = even[y + 1, i + 1, pl.ds(nz - 1, 1)]
            z_out[0, 1, y, pl.ds(i, 1)] = even[y + 1, i + 1, pl.ds(0, 1)]

    each(nx, pack)
    start(z_copies(0))
    loads[1].wait()
    loads[2].wait()

    row = lax.broadcasted_iota(jnp.int32, (nz, 128), 0)

    def one_line(n, y, i):
        old, new = (odd, even) if n % 2 else (even, odd)
        middle = old[y + 1, i + 1]
        low = jnp.where(row == 0, z_low[n, y, pl.ds(i, 1)], pltpu.roll(middle, 1, 0))
        high = jnp.where(row == nz - 1, z_high[n, y, pl.ds(i, 1)], pltpu.roll(middle, nz - 1, 0))
        spread = old[y, i + 1] + old[y + 2, i + 1] + old[y + 1, i] + old[y + 1, i + 2] + low + high - 6.0 * middle
        value = middle + mob[y, i] * spread + src[y, i]
        new[y + 1, i + 1] = value
        if n + 1 < STEPS:
            z_out[n + 1, 0, y, pl.ds(i, 1)] = value[nz - 1:]
            z_out[n + 1, 1, y, pl.ds(i, 1)] = value[:1]
        return value

    def line_stats(value, c, k, y):
        mean = jnp.sum(value, axis=0, keepdims=True) * (1.0 / nz)
        centred = value - mean
        at = pl.ds(k * ny + y, 1)
        stats[0, c, 0, at] = mean
        stats[0, c, 1, at] = jnp.sum(centred * centred, axis=0, keepdims=True)

    for n in range(STEPS - 1):
        arrived(x_copies(n))
        arrived(z_copies(n))

        def inner(i):
            for y in range(1, ny - 1):
                one_line(n, y, i)

        def outer(c):
            arrived(y_copies(n, c))
            for k in range(LINES):
                for y in (0, ny - 1):
                    one_line(n, y, c * LINES + k)

        def outer_and_send(c):
            outer(c)
            start(y_copies(n + 1, c - 1))

        each(nx, inner)
        outer(0)
        lax.fori_loop(1, pieces, lambda c, carry: (outer_and_send(c), carry)[1], 0)
        start(x_copies(n + 1))
        start(z_copies(n + 1))
        start(y_copies(n + 1, pieces - 1))

    n = STEPS - 1
    sent(x_copies(n - 1))
    arrived(x_copies(n))
    arrived(z_copies(n))

    def last(c):
        sent(y_copies(n - 1, c))
        for k in range(LINES):
            for y in range(1, ny - 1):
                line_stats(one_line(n, y, c * LINES + k), c, k, y)
        arrived(y_copies(n, c))
        for k in range(LINES):
            for y in (0, ny - 1):
                line_stats(one_line(n, y, c * LINES + k), c, k, y)
        start(stat_copies(c))

    each(pieces, last)

    sent(x_copies(0))
    sent(x_copies(n))
    for m in range(STEPS):
        sent(z_copies(m))

    def drain(c):
        sent(y_copies(0, c))
        sent(y_copies(n, c))
        sent(stat_copies(c))
        arrived(stat_copies(c))

    each(pieces, drain)


def finish_kernel(field, stats, anomaly, field_end, held, sems):
    slabs, pieces, _, rows, _ = stats.shape
    ny, nx, nz, _ = field_end.shape
    whole = [
        pltpu.make_async_copy(field.at[y + 1, pl.ds(1, nx)], field_end.at[y], sems.at[y]) for y in range(ny)
    ]
    for copy in whole:
        copy.start()

    def copy_of(c):
        lines = pl.ds(c * LINES, LINES)
        return pltpu.make_async_copy(held.at[:, lines], anomaly.at[:, lines], sems.at[ny + c])

    def piece(c, carry):
        means = [stats[d, c, 0] for d in range(slabs)]
        mean = sum(means[1:], means[0]) * (1.0 / slabs)
        spread = stats[0, c, 1]
        for d in range(1, slabs):
            spread = spread + stats[d, c, 1]
        for other in means:
            spread = spread + (other - mean) * (other - mean) * float(nz)
        scale = lax.rsqrt(spread * (1.0 / (nz * slabs)) + EPS)
        for k in range(LINES):
            for y in range(ny):
                r = k * ny + y
                i = c * LINES + k
                held[y, i] = (field[y + 1, i + 1] - mean[r:r + 1]) * scale[r:r + 1]
        copy_of(c).start()
        return carry

    lax.fori_loop(0, pieces, piece, 0)
    for copy in whole:
        copy.wait()
    lax.fori_loop(0, pieces, lambda c, carry: (copy_of(c).wait(), carry)[1], 0)


def per_device(field, mobility, source):
    ny, nx, nz, levels = field.shape
    f32 = jnp.float32
    pieces = nx // LINES
    slabs = lax.axis_size("slabs")
    any_space = pl.BlockSpec(memory_space=pl.ANY)
    vmem = pl.BlockSpec(memory_space=pltpu.VMEM)
    padded = (ny + 2, nx + 2, nz, levels)
    faces = (STEPS, ny, nx, levels)
    end, stats = pl.pallas_call(
        steps_kernel,
        out_shape=(pltpu.VMEM(padded, f32), pltpu.VMEM((slabs, pieces, 2, LINES * ny, levels), f32)),
        in_specs=[any_space] * 3,
        out_specs=(vmem, vmem),
        scratch_shapes=[
            pltpu.VMEM(padded, f32),
            pltpu.VMEM(field.shape, f32),
            pltpu.VMEM(field.shape, f32),
            pltpu.VMEM(faces, f32),
            pltpu.VMEM(faces, f32),
            pltpu.VMEM((STEPS, 2, ny, nx, levels), f32),
            DMA((STEPS, 2, pieces)),
            DMA((STEPS, 2, pieces)),
            DMA((STEPS, 2)),
            DMA((STEPS, 2)),
            DMA((STEPS, 2)),
            DMA((STEPS, 2)),
            DMA((slabs - 1, pieces)),
            DMA((slabs - 1, pieces)),
            DMA((3,)),
        ],
        name="steps",
        compiler_params=pltpu.CompilerParams(
            collective_id=0, has_side_effects=True, vmem_limit_bytes=46 * 2**20
        ),
    )(field, mobility, source)
    shape = jax.ShapeDtypeStruct(field.shape, f32)
    return pl.pallas_call(
        finish_kernel,
        out_shape=(shape, shape),
        in_specs=[vmem, vmem],
        out_specs=(any_space, any_space),
        scratch_shapes=[pltpu.VMEM(field.shape, f32), DMA((ny + pieces,))],
        name="finish",
        compiler_params=pltpu.CompilerParams(vmem_limit_bytes=24 * 2**20),
    )(end, stats)


def solution(mesh):
    spec = P("rows", "cols", "slabs", None)
    return jax.shard_map(
        per_device, mesh=mesh, in_specs=(spec,) * 3, out_specs=(spec, spec), check_vma=False
    )
```

time: 268 us -> 156 us (0.58)
  Pallas kernels: 0 us -> 155 us
  waiting for transfers between devices: 103 us -> 0 us
  other arithmetic: 92.2 us -> 0 us
  starting transfers between devices: 33.8 us -> 0 us
  local copies, waits for them, and re-layouts: 24 us -> 0 us
  blocking collectives: 12.7 us -> 0 us
    pallas_call x0 -> x2, Pallas kernels: none -> 155 us  [the longest x1 149 us: per_device(): pl.pallas_call(steps_kernel, out_shape=(pltpu.VMEM(padded, f32), pltpu.VM...]
    ppermute x18 -> x0, waiting for transfers between devices: 103 us -> none  [the longest x9 99.8 us: padded_2(): lax.ppermute(last, axis, up)]
    add x3 -> x0, other arithmetic: 54.2 us -> none  [the longest x2 54.2 us: one_step(): return middle + mobility * spread + source]
    ppermute x18 -> x0, starting transfers between devices: 33.8 us -> none  [the longest x9 25.5 us: padded_2(): lax.ppermute(initial, axis, [(b, a) for a, b in up])]
    reduce_sum x2 -> x0, other arithmetic: 29.2 us -> none  [the longest x1 28.7 us: per_device(): jnp.sum(moved, axis=2, keepdims=True)]
    slice x9 -> x0, local copies, waits for them, and re-layouts: 14.5 us -> none  [the longest x8 10.5 us: padded_2(): last = lax.slice_in_dim(shard, length - width, length, axis=dim)]
    all_to_all x1 -> x0, blocking collectives: 12.7 us -> none  [copy_for_each(): return lax.all_to_all(copies, axis, split_axis=0, concat_axis=0, tiled=True)]
    mul x1 -> x0, other arithmetic: 8.85 us -> none  [per_device(): anomaly = centred * lax.rsqrt(line_variance + 0.0001)]
  transfers between devices with their start and end apart: 18 -> 0, of which waited for: 8 -> 0; matrix products, arithmetic and copies ran while one was open for 5% -> 0% of each run, Pallas kernels for 0% -> 0%
where the time goes in v1:
time: 156 us; the launch traced here: 155 us
  Pallas kernels  155 us (99%)
    pallas_call x1, Pallas kernels, per_device(): pl.pallas_call(steps_kernel, out_shape=(pltpu.VMEM(padded, f32), pltpu.VM...  149 us
    pallas_call x1, Pallas kernels, per_device(): pl.pallas_call(finish_kernel, out_shape=(shape, shape), in_specs=[vmem, v...  5.98 us

profile of v1, /device:TPU:0, one launch (start us, length us, event | category | flops | bytes accessed | tf_op | source)
XLA Modules:
  0.0 155.4 jit_solution(177995292878297745)
XLA Ops:
  0.6 148.8 %steps.1 = (f32[6,34,128,128]{3,2,1,0:T(8,128)S(1)}, f32[4,16,2,8,128]{4,3,2,1,0:T(8,128)S(1)}) custom-call(f32[4,32,128,128]{3,2,1,0:T(8,128)} %field.1, f32[4,32,128,128]{3,2,1,0:T(8,128)} %mobility.1, f32[4,32,128,128]{3,2,1,0:T(8,128)} %source.1), custom_call_target="tpu_custom_call" | custom-call | tf_op jit(solution)/shard_map/steps/pallas_call | solution.py:244
  149.5 6.0 %finish.1 = (f32[4,32,128,128]{3,2,1,0:T(8,128)}, f32[4,32,128,128]{3,2,1,0:T(8,128)}) custom-call(f32[6,34,128,128]{3,2,1,0:T(8,128)S(1)} %get-tuple-element.4.field, f32[4,16,2,8,128]{4,3,2,1,0:T(8,128)S(1)} %get-tuple-element.5.stats), custom_call_target="tpu_custom_call" | custom-call | tf_op jit(solution)/shard_map/finish/pallas_call | solution.py:272

commit v2 on v1

v2 whole, which is shorter than its diff:
```python
import jax
import jax.numpy as jnp
from jax import lax
from jax.experimental import pallas as pl
from jax.experimental.pallas import tpu as pltpu
from jax.sharding import PartitionSpec as P

STEPS = 3
LINES = (4, 4, 4)
L = LINES[-1]
LEAVE = (7, 4)
HOLD = 1
EPS = 1e-4
MESH = pl.DeviceIdType.MESH
DMA = pltpu.SemaphoreType.DMA


def ring(axis, by):
    size = lax.axis_size(axis)
    return {axis: lax.rem(lax.axis_index(axis) + by % size, size)}


def remote(src, dst, send, recv, to):
    return pltpu.make_async_remote_copy(
        src_ref=src, dst_ref=dst, send_sem=send, recv_sem=recv, device_id=to, device_id_type=MESH
    )


def start(copies):
    for copy in copies:
        copy.start()


def wait(copies):
    for copy in copies:
        copy.wait()


def arrived(copies):
    for copy in copies:
        copy.wait_recv()


def sent(copies):
    for copy in copies:
        copy.wait_send()


def each(first, end, body):
    def step(i, carry):
        body(i)
        return carry

    lax.fori_loop(first, end, step, 0)


def leaving():
    return LEAVE[0] + (LEAVE[1] - LEAVE[0]) * lax.rem(lax.axis_index("cols"), 2)


def greet(peers):
    barrier = pltpu.get_barrier_semaphore()
    for peer in peers:
        pl.semaphore_signal(barrier, inc=1, device_id=peer, device_id_type=MESH)
    return lambda: pl.semaphore_wait(barrier, len(peers))


def others():
    return [ring("slabs", d) for d in range(1, lax.axis_size("slabs"))]


def next_value(middle, below, above, left, right, low_row, high_row, mobility, source):
    nz = middle.shape[0]
    row = lax.broadcasted_iota(jnp.int32, middle.shape, 0)
    low = jnp.where(row == 0, low_row, pltpu.roll(middle, 1, 0))
    high = jnp.where(row == nz - 1, high_row, pltpu.roll(middle, nz - 1, 0))
    return middle + mobility * (below + above + left + right + low + high - 6.0 * middle) + source


def line_stats(stats, value, c, r):
    nz = value.shape[0]
    mean = jnp.sum(value, axis=0, keepdims=True) * (1.0 / nz)
    centred = value - mean
    stats[0, c, 0, pl.ds(r, 1)] = mean
    stats[0, c, 1, pl.ds(r, 1)] = jnp.sum(centred * centred, axis=0, keepdims=True)


def stat_copies(stats, s_send, s_recv, c):
    return [
        remote(stats.at[0, c], stats.at[d, c], s_send.at[d - 1, c], s_recv.at[d - 1, c], ring("slabs", d))
        for d in range(1, lax.axis_size("slabs"))
    ]


def first_kernel(
    field, mobility, source, odd, even, z_end, stats,
    mob, src, z_in, z_out,
    y_send, y_recv, x_send, x_recv, z_send, z_recv, s_send, s_recv, local,
):
    ny, nx, nz, _ = field.shape
    pieces = [nx // lines for lines in LINES]
    leave = leaving()

    def load(y, planes, first, lines, sem):
        return pltpu.make_async_copy(
            field.at[pl.ds(y, planes), pl.ds(first, lines)],
            even.at[pl.ds(y + 1, planes), pl.ds(first + 1, lines)],
            local.at[sem],
        )

    ahead = [load(0, 1, 0, LINES[0], 0), load(ny - 1, 1, 0, LINES[0], 1)]
    loads = [
        load(0, 1, LINES[0], nx - LINES[0], 2),
        load(ny - 1, 1, LINES[0], nx - LINES[0], 3),
        load(1, ny - 2, 0, nx, 4),
    ]
    more = [
        pltpu.make_async_copy(mobility, mob, local.at[5]),
        pltpu.make_async_copy(source, src, local.at[6]),
    ]
    met = greet([ring("rows", 1), ring("rows", -1), ring("cols", 1), ring("cols", -1)] + others())
    start(ahead + loads + more)
    wait(ahead)
    met()

    def y_copies(n, c):
        buf = odd if n % 2 else even
        lines = pl.ds(1 + c * LINES[n], LINES[n])
        if n or (isinstance(c, int) and c == 0):
            first, last = buf.at[1, lines], buf.at[ny, lines]
        else:
            here = pl.ds(c * LINES[n], LINES[n])
            first, last = field.at[0, here], field.at[ny - 1, here]
        return (
            remote(last, buf.at[0, lines], y_send.at[n, 0, c], y_recv.at[n, 0, c], ring("rows", 1)),
            remote(first, buf.at[ny + 1, lines], y_send.at[n, 1, c], y_recv.at[n, 1, c], ring("rows", -1)),
        )

    def x_copies(n):
        buf = odd if n % 2 else even
        planes = pl.ds(1, ny)
        if n:
            first, last = buf.at[planes, 1], buf.at[planes, nx]
        else:
            first, last = field.at[:, 0], field.at[:, nx - 1]
        return (
            remote(last, buf.at[planes, 0], x_send.at[n, 0], x_recv.at[n, 0], ring("cols", 1)),
            remote(first, buf.at[planes, nx + 1], x_send.at[n, 1], x_recv.at[n, 1], ring("cols", -1)),
        )

    def z_faces(n):
        return z_in.at[n] if n + 1 < STEPS else z_end

    def z_copies(n):
        return (
            remote(z_out.at[n, 0], z_faces(n).at[0], z_send.at[n, 0], z_recv.at[n, 0], ring("slabs", 1)),
            remote(z_out.at[n, 1], z_faces(n).at[1], z_send.at[n, 1], z_recv.at[n, 1], ring("slabs", -1)),
        )

    start(y_copies(0, 0))
    each(1, pieces[0], lambda c: start(y_copies(0, c)))
    start(x_copies(0))
    wait(loads)

    def pack(i):
        for y in range(ny):
            z_out[0, 0, y, pl.ds(i, 1)] = even[y + 1, i + 1, pl.ds(nz - 1, 1)]
            z_out[0, 1, y, pl.ds(i, 1)] = even[y + 1, i + 1, pl.ds(0, 1)]

    each(0, nx, pack)
    start(z_copies(0))
    wait(more)

    def one_line(n, y, i):
        old, new = (odd, even) if n % 2 else (even, odd)
        faces = z_faces(n)
        value = next_value(
            old[y + 1, i + 1], old[y, i + 1], old[y + 2, i + 1], old[y + 1, i], old[y + 1, i + 2],
            faces[0, y, pl.ds(i, 1)], faces[1, y, pl.ds(i, 1)], mob[y, i], src[y, i],
        )
        new[y + 1, i + 1] = value
        if n + 1 < STEPS:
            z_out[n + 1, 0, y, pl.ds(i, 1)] = value[nz - 1:]
            z_out[n + 1, 1, y, pl.ds(i, 1)] = value[:1]
        return value

    def send_piece(n, c):
        if n + 1 < STEPS:
            start(y_copies(n, c))
            return
        parts = LINES[n - 1] // LINES[n]
        for part in range(parts):

            @pl.when(c * parts + part < leave)
            def _():
                start(y_copies(n, c * parts + part))

    for n in range(STEPS - 1):
        if n == 1:
            sent(y_copies(0, 0))
        arrived(x_copies(n))
        arrived(z_copies(n))

        def inner(i):
            for y in range(1, ny - 1):
                one_line(n, y, i)

        def outer(c):
            arrived(y_copies(n, c))

            def line(k):
                for y in (0, ny - 1):
                    one_line(n, y, c * LINES[n] + k)

            each(0, LINES[n], line)

        def outer_and_send(c):
            outer(c)
            send_piece(n + 1, c - 1)

        each(0, nx, inner)
        outer(0)
        each(1, pieces[n], outer_and_send)
        start(x_copies(n + 1))
        start(z_copies(n + 1))
        send_piece(n + 1, pieces[n] - 1)

    n = STEPS - 1
    each(0, pieces[n - 1], lambda c: sent(y_copies(n - 1, c)))
    sent(x_copies(n - 1))
    arrived(x_copies(n))
    arrived(z_copies(n))

    def last(c):
        for k in range(L):
            for y in range(1, ny - 1):
                line_stats(stats, one_line(n, y, c * L + k), c, k * ny + y)
        arrived(y_copies(n, c))
        for k in range(L):
            for y in (0, ny - 1):
                line_stats(stats, one_line(n, y, c * L + k), c, k * ny + y)
        start(stat_copies(stats, s_send, s_recv, c))

    each(0, leave - HOLD, last)
    each(leave - HOLD, leave, lambda c: arrived(y_copies(n, c)))
    each(0, leave, lambda c: sent(y_copies(n, c)))
    each(1, pieces[0], lambda c: sent(y_copies(0, c)))
    sent(x_copies(0))
    sent(x_copies(n))
    for m in range(STEPS):
        sent(z_copies(m))

    def drain(c):
        sent(stat_copies(stats, s_send, s_recv, c))
        arrived(stat_copies(stats, s_send, s_recv, c))

    each(0, leave - HOLD, drain)


def second_kernel(
    even, z_end, mobility, source, after, rest, stats,
    mob, src, halo, y_send, y_recv, s_send, s_recv, local,
):
    ny, nx, nz, _ = mobility.shape
    pieces = nx // L
    leave = leaving()
    begin = leave - HOLD

    def loads(c):
        there, here = pl.ds(c * L, L), pl.ds((c - begin) * L, L)
        return (
            pltpu.make_async_copy(mobility.at[:, there], mob.at[:, here], local.at[0, c - begin]),
            pltpu.make_async_copy(source.at[:, there], src.at[:, here], local.at[1, c - begin]),
        )

    def y_copies(c):
        lines, landing = pl.ds(1 + c * L, L), pl.ds((c - leave) * L, L)
        p = c - leave
        return (
            remote(even.at[ny, lines], halo.at[0, landing], y_send.at[0, p], y_recv.at[0, p], ring("rows", 1)),
            remote(even.at[1, lines], halo.at[1, landing], y_send.at[1, p], y_recv.at[1, p], ring("rows", -1)),
        )

    def my_stats(c):
        return stat_copies(stats, s_send, s_recv, c - begin)

    met = greet([ring("rows", 1), ring("rows", -1)] + others())
    each(begin, pieces, lambda c: start(loads(c)))
    met()
    each(leave, pieces, lambda c: start(y_copies(c)))

    def one_line(c, k, y, landed):
        i = c * L + k
        r = (c - begin) * L + k
        below = halo[0, (c - leave) * L + k] if landed and y == 0 else even[y, i + 1]
        above = halo[1, (c - leave) * L + k] if landed and y == ny - 1 else even[y + 2, i + 1]
        value = next_value(
            even[y + 1, i + 1], below, above, even[y + 1, i], even[y + 1, i + 2],
            z_end[0, y, pl.ds(i, 1)], z_end[1, y, pl.ds(i, 1)], mob[y, r], src[y, r],
        )
        rest[y, r] = value
        line_stats(stats, value, c - begin, k * ny + y)

    def inner(c, landed):
        wait(loads(c))
        for k in range(L):
            for y in range(1, ny - 1):
                one_line(c, k, y, landed)

    def outer(c, landed):
        for k in range(L):
            for y in (0, ny - 1):
                one_line(c, k, y, landed)
        start(my_stats(c))

    def held(c):
        inner(c, False)
        outer(c, False)

    def moved(c):
        inner(c, True)
        arrived(y_copies(c))
        outer(c, True)

    each(begin, leave, held)
    each(leave, pieces, moved)
    each(leave, pieces, lambda c: sent(y_copies(c)))

    def drain(c):
        sent(my_stats(c))
        arrived(my_stats(c))

    each(begin, pieces, drain)


def write_pieces(first, end, stats_of, value_of, block_of, anomaly, field_end, held, sems):
    ny, _, nz, _ = field_end.shape

    def field_copy(c):
        return pltpu.make_async_copy(block_of(c), field_end.at[:, pl.ds(c * L, L)], sems.at[0, c])

    def anomaly_copy(c):
        lines = pl.ds(c * L, L)
        return pltpu.make_async_copy(held.at[:, lines], anomaly.at[:, lines], sems.at[1, c])

    def piece(c):
        stats = stats_of(c)
        slabs = len(stats)
        mean = sum((a for a, _ in stats[1:]), stats[0][0]) * (1.0 / slabs)
        spread = sum((b for _, b in stats[1:]), stats[0][1])
        for a, _ in stats:
            spread = spread + (a - mean) * (a - mean) * float(nz)
        scale = lax.rsqrt(spread * (1.0 / (nz * slabs)) + EPS)
        for k in range(L):
            for y in range(ny):
                r = k * ny + y
                held[y, c * L + k] = (value_of(c, k, y) - mean[r:r + 1]) * scale[r:r + 1]
        anomaly_copy(c).start()

    each(first, end, lambda c: field_copy(c).start())
    each(first, end, piece)

    def done(c):
        field_copy(c).wait()
        anomaly_copy(c).wait()

    each(first, end, done)


def first_write(odd, stats, anomaly, field_end, after, held, sems):
    ny = field_end.shape[0]
    slabs = stats.shape[0]
    write_pieces(
        0, leaving() - HOLD,
        lambda c: [(stats[d, c, 0], stats[d, c, 1]) for d in range(slabs)],
        lambda c, k, y: odd[y + 1, c * L + k + 1],
        lambda c: odd.at[pl.ds(1, ny), pl.ds(c * L + 1, L)],
        anomaly, field_end, held, sems,
    )
    after[...] = jnp.zeros_like(after)


def second_write(rest, stats, _a, _f, anomaly, field_end, held, sems):
    slabs = stats.shape[0]
    begin = leaving() - HOLD
    write_pieces(
        begin, field_end.shape[1] // L,
        lambda c: [(stats[d, c - begin, 0], stats[d, c - begin, 1]) for d in range(slabs)],
        lambda c, k, y: rest[y, (c - begin) * L + k],
        lambda c: rest.at[:, pl.ds((c - begin) * L, L)],
        anomaly, field_end, held, sems,
    )


def near(x):
    return pltpu.with_memory_space_constraint(x, pltpu.VMEM)


def far(x):
    return pltpu.with_memory_space_constraint(x, pltpu.HBM)


def per_device(field, mobility, source):
    ny, nx, nz, levels = field.shape
    f32 = jnp.float32
    pieces = nx // L
    most = nx // min(LINES)
    slabs = lax.axis_size("slabs")
    any_space = pl.BlockSpec(memory_space=pl.ANY)
    vmem = pl.BlockSpec(memory_space=pltpu.VMEM)
    padded = (ny + 2, nx + 2, nz, levels)
    faces = (2, ny, nx, levels)
    left = pieces - min(LEAVE) + HOLD
    coming = pieces - min(LEAVE)
    odd, even, z_end, stats = pl.pallas_call(
        first_kernel,
        out_shape=(
            pltpu.VMEM(padded, f32),
            pltpu.VMEM(padded, f32),
            pltpu.VMEM(faces, f32),
            pltpu.VMEM((slabs, pieces, 2, L * ny, levels), f32),
        ),
        in_specs=[any_space] * 3,
        out_specs=(vmem,) * 4,
        scratch_shapes=[
            pltpu.VMEM(field.shape, f32),
            pltpu.VMEM(field.shape, f32),
            pltpu.VMEM((STEPS - 1, *faces), f32),
            pltpu.VMEM((STEPS, *faces), f32),
            DMA((STEPS, 2, most)),
            DMA((STEPS, 2, most)),
            DMA((STEPS, 2)),
            DMA((STEPS, 2)),
            DMA((STEPS, 2)),
            DMA((STEPS, 2)),
            DMA((slabs - 1, pieces)),
            DMA((slabs - 1, pieces)),
            DMA((7,)),
        ],
        name="steps",
        compiler_params=pltpu.CompilerParams(
            collective_id=0, has_side_effects=True, vmem_limit_bytes=22 * 2**20
        ),
    )(field, mobility, source)
    shape = jax.ShapeDtypeStruct(field.shape, f32)
    writing = dict(
        scratch_shapes=[pltpu.VMEM(field.shape, f32), DMA((2, pieces))],
        compiler_params=pltpu.CompilerParams(vmem_limit_bytes=12 * 2**20),
    )
    anomaly, field_end, after = pl.pallas_call(
        first_write,
        out_shape=(shape, shape, jax.ShapeDtypeStruct((8, levels), f32)),
        in_specs=[vmem, vmem],
        out_specs=(any_space, any_space, vmem),
        name="write",
        **writing,
    )(near(odd), near(stats))
    rest, stats = pl.pallas_call(
        second_kernel,
        out_shape=(
            pltpu.VMEM((ny, left * L, nz, levels), f32),
            pltpu.VMEM((slabs, left, 2, L * ny, levels), f32),
        ),
        in_specs=[vmem, vmem, any_space, any_space, any_space],
        out_specs=(vmem, vmem),
        scratch_shapes=[
            pltpu.VMEM((ny, left * L, nz, levels), f32),
            pltpu.VMEM((ny, left * L, nz, levels), f32),
            pltpu.VMEM((2, coming * L, nz, levels), f32),
            DMA((2, coming)),
            DMA((2, coming)),
            DMA((slabs - 1, left)),
            DMA((slabs - 1, left)),
            DMA((2, left)),
        ],
        name="rest",
        compiler_params=pltpu.CompilerParams(
            collective_id=1, has_side_effects=True, vmem_limit_bytes=16 * 2**20
        ),
    )(near(even), near(z_end), far(mobility), far(source), after)
    return pl.pallas_call(
        second_write,
        out_shape=(shape, shape),
        in_specs=[vmem, vmem, any_space, any_space],
        out_specs=(any_space, any_space),
        input_output_aliases={2: 0, 3: 1},
        name="write_rest",
        **writing,
    )(near(rest), near(stats), anomaly, field_end)


def solution(mesh):
    spec = P("rows", "cols", "slabs", None)
    return jax.shard_map(
        per_device, mesh=mesh, in_specs=(spec,) * 3, out_specs=(spec, spec), check_vma=False
    )
```

time: 156 us -> 152 us (0.974)
  Pallas kernels: 155 us -> 151 us
    pallas_call x2 -> x4, Pallas kernels: 155 us -> 151 us  [the longest x1 131 us: per_device(): pl.pallas_call(first_kernel, out_shape=(pltpu.VMEM(padded, f32), pltpu.VM...]
where the time goes in v2:
time: 152 us
  Pallas kernels  151 us (99%)
    pallas_call x1, Pallas kernels, per_device(): pl.pallas_call(first_kernel, out_shape=(pltpu.VMEM(padded, f32), pltpu.VM...  131 us
    pallas_call x1, Pallas kernels, per_device(): pl.pallas_call(second_kernel, out_shape=(pltpu.VMEM((ny, left * L, nz, le...  13.2 us
    pallas_call x1, Pallas kernels, per_device(): pl.pallas_call(first_write, out_shape=(shape, shape, jax.ShapeDtypeStruct...  4.72 us

profile of v2, /device:TPU:0, one launch (start us, length us, event | category | flops | bytes accessed | tf_op | source)
XLA Modules:
  0.0 151.6 jit_solution(8773293672497272053)
XLA Ops:
  0.6 130.9 %steps.1 = (f32[6,34,128,128]{3,2,1,0:T(8,128)S(1)}, f32[6,34,128,128]{3,2,1,0:T(8,128)S(1)}, f32[2,4,32,128]{3,2,1,0:T(8,128)S(1)}, f32[4,8,2,16,128]{4,3,2,1,0:T(8,128)S(1)}) custom-call(f32[4,32,128,128]{3,2,1,0:T(8,128)} %field.1, f32[4,32,128,128]{3,2,1,0:T(8,128)} %mobility.3, f32[4,32,128,128]{3,2,1,0:T(8,128)} %source.3), custom_call_target="tpu_custom_call" | custom-call | tf_op jit(solution)/shard_map/steps/pallas_call | solution.py:415
  131.5 4.7 %write.1 = (f32[4,32,128,128]{3,2,1,0:T(8,128)}, f32[4,32,128,128]{3,2,1,0:T(8,128)}, f32[8,128]{1,0:T(8,128)S(1)}) custom-call(f32[6,34,128,128]{3,2,1,0:T(8,128)S(1)} %get-tuple-element.13.odd, f32[4,8,2,16,128]{4,3,2,1,0:T(8,128)S(1)} %get-tuple-element.14.stats), custom_call_target="tpu_custom_call" | custom-call | tf_op jit(solution)/shard_map/write/pallas_call | solution.py:450
  136.3 13.2 %rest.1 = (f32[4,20,128,128]{3,2,1,0:T(8,128)S(1)}, f32[4,5,2,16,128]{4,3,2,1,0:T(8,128)S(1)}) custom-call(f32[6,34,128,128]{3,2,1,0:T(8,128)S(1)} %get-tuple-element.11.even, f32[2,4,32,128]{3,2,1,0:T(8,128)S(1)} %get-tuple-element.12.z_end, f32[4,32,128,128]{3,2,1,0:T(8,128)} %mobility.3, f32[4,32,128,128]{3,2,1,0:T(8,128)} %source.3, ...), custom_call_target="tpu_custom_call" | custom-call | tf_op jit(solution)/shard_map/rest/pallas_call | solution.py:458
  149.5 2.2 %write_rest.1 = (f32[4,32,128,128]{3,2,1,0:T(8,128)}, f32[4,32,128,128]{3,2,1,0:T(8,128)}) custom-call(f32[4,20,128,128]{3,2,1,0:T(8,128)S(1)} %get-tuple-element.16.rest, f32[4,5,2,16,128]{4,3,2,1,0:T(8,128)S(1)} %get-tuple-element.17.stats, f32[4,32,128,128]{3,2,1,0:T(8,128)} %get-tuple-element.18._a, ...), custom_call_target="tpu_custom_call", output_to_operand_aliasing={{0}: (2, {}), {1}: (3, {})} | custom-call | tf_op jit(solution)/shard_map/write_rest/pallas_call | solution.py:481

commit v3 on v2

--- a/solution.py
+++ b/solution.py
@@ -8,8 +8,9 @@
 STEPS = 3
 LINES = (4, 4, 4)
 L = LINES[-1]
-LEAVE = (7, 4)
-HOLD = 1
+LEAVE = (7, 3)
+HOLD = (1, 1)
+INNER = (1, 2)
 EPS = 1e-4
 MESH = pl.DeviceIdType.MESH
 DMA = pltpu.SemaphoreType.DMA
@@ -54,8 +55,16 @@
     lax.fori_loop(first, end, step, 0)
 
 
+def by_core(values):
+    return values[0] + (values[1] - values[0]) * lax.rem(lax.axis_index("cols"), 2)
+
+
 def leaving():
-    return LEAVE[0] + (LEAVE[1] - LEAVE[0]) * lax.rem(lax.axis_index("cols"), 2)
+    return by_core(LEAVE)
+
+
+def beginning():
+    return by_core([leave - hold for leave, hold in zip(LEAVE, HOLD)])
 
 
 def greet(peers):
@@ -93,13 +102,14 @@
 
 
 def first_kernel(
-    field, mobility, source, odd, even, z_end, stats,
+    field, mobility, source, odd, even, z_end, inner_stats, outer_stats,
     mob, src, z_in, z_out,
-    y_send, y_recv, x_send, x_recv, z_send, z_recv, s_send, s_recv, local,
+    y_send, y_recv, x_send, x_recv, z_send, z_recv, i_send, i_recv, s_send, s_recv, local,
 ):
     ny, nx, nz, _ = field.shape
     pieces = [nx // lines for lines in LINES]
     leave = leaving()
+    begin = beginning()
 
     def load(y, planes, first, lines, sem):
         return pltpu.make_async_copy(
@@ -231,18 +241,28 @@
     arrived(x_copies(n))
     arrived(z_copies(n))
 
+    def all_inner_stats():
+        return [
+            remote(inner_stats.at[0], inner_stats.at[d], i_send.at[d - 1], i_recv.at[d - 1], ring("slabs", d))
+            for d in range(1, lax.axis_size("slabs"))
+        ]
+
+    def inner_piece(c):
+        for k in range(L):
+            for p, y in enumerate(INNER):
+                line_stats(inner_stats, one_line(n, y, c * L + k), c, 2 * k + p)
+
     def last(c):
-        for k in range(L):
-            for y in range(1, ny - 1):
-                line_stats(stats, one_line(n, y, c * L + k), c, k * ny + y)
         arrived(y_copies(n, c))
         for k in range(L):
-            for y in (0, ny - 1):
-                line_stats(stats, one_line(n, y, c * L + k), c, k * ny + y)
-        start(stat_copies(stats, s_send, s_recv, c))
-
-    each(0, leave - HOLD, last)
-    each(leave - HOLD, leave, lambda c: arrived(y_copies(n, c)))
+            for p, y in enumerate((0, ny - 1)):
+                line_stats(outer_stats, one_line(n, y, c * L + k), c, 2 * k + p)
+        start(stat_copies(outer_stats, s_send, s_recv, c))
+
+    each(0, pieces[n], inner_piece)
+    start(all_inner_stats())
+    each(0, begin, last)
+    each(begin, leave, lambda c: arrived(y_copies(n, c)))
     each(0, leave, lambda c: sent(y_copies(n, c)))
     each(1, pieces[0], lambda c: sent(y_copies(0, c)))
     sent(x_copies(0))
@@ -251,10 +271,12 @@
         sent(z_copies(m))
 
     def drain(c):
-        sent(stat_copies(stats, s_send, s_recv, c))
-        arrived(stat_copies(stats, s_send, s_recv, c))
-
-    each(0, leave - HOLD, drain)
+        sent(stat_copies(outer_stats, s_send, s_recv, c))
+        arrived(stat_copies(outer_stats, s_send, s_recv, c))
+
+    each(0, begin, drain)
+    sent(all_inner_stats())
+    arrived(all_inner_stats())
 
 
 def second_kernel(
@@ -264,14 +286,15 @@
     ny, nx, nz, _ = mobility.shape
     pieces = nx // L
     leave = leaving()
-    begin = leave - HOLD
+    begin = beginning()
 
     def loads(c):
         there, here = pl.ds(c * L, L), pl.ds((c - begin) * L, L)
-        return (
-            pltpu.make_async_copy(mobility.at[:, there], mob.at[:, here], local.at[0, c - begin]),
-            pltpu.make_async_copy(source.at[:, there], src.at[:, here], local.at[1, c - begin]),
-        )
+        return [
+            pltpu.make_async_copy(whole.at[y, there], part.at[p, here], local.at[q, p, c - begin])
+            for q, (whole, part) in enumerate(((mobility, mob), (source, src)))
+            for p, y in enumerate((0, ny - 1))
+        ]
 
     def y_copies(c):
         lines, landing = pl.ds(1 + c * L, L), pl.ds((c - leave) * L, L)
@@ -284,112 +307,114 @@
     def my_stats(c):
         return stat_copies(stats, s_send, s_recv, c - begin)
 
-    met = greet([ring("rows", 1), ring("rows", -1)] + others())
-    each(begin, pieces, lambda c: start(loads(c)))
-    met()
-    each(leave, pieces, lambda c: start(y_copies(c)))
-
-    def one_line(c, k, y, landed):
-        i = c * L + k
-        r = (c - begin) * L + k
-        below = halo[0, (c - leave) * L + k] if landed and y == 0 else even[y, i + 1]
-        above = halo[1, (c - leave) * L + k] if landed and y == ny - 1 else even[y + 2, i + 1]
-        value = next_value(
-            even[y + 1, i + 1], below, above, even[y + 1, i], even[y + 1, i + 2],
-            z_end[0, y, pl.ds(i, 1)], z_end[1, y, pl.ds(i, 1)], mob[y, r], src[y, r],
-        )
-        rest[y, r] = value
-        line_stats(stats, value, c - begin, k * ny + y)
-
-    def inner(c, landed):
-        wait(loads(c))
-        for k in range(L):
-            for y in range(1, ny - 1):
-                one_line(c, k, y, landed)
-
-    def outer(c, landed):
-        for k in range(L):
-            for y in (0, ny - 1):
-                one_line(c, k, y, landed)
-        start(my_stats(c))
-
-    def held(c):
-        inner(c, False)
-        outer(c, False)
-
-    def moved(c):
-        inner(c, True)
-        arrived(y_copies(c))
-        outer(c, True)
-
-    each(begin, leave, held)
-    each(leave, pieces, moved)
-    each(leave, pieces, lambda c: sent(y_copies(c)))
-
-    def drain(c):
-        sent(my_stats(c))
-        arrived(my_stats(c))
-
-    each(begin, pieces, drain)
-
-
-def write_pieces(first, end, stats_of, value_of, block_of, anomaly, field_end, held, sems):
-    ny, _, nz, _ = field_end.shape
-
-    def field_copy(c):
-        return pltpu.make_async_copy(block_of(c), field_end.at[:, pl.ds(c * L, L)], sems.at[0, c])
-
-    def anomaly_copy(c):
+    @pl.when(begin < pieces)
+    def _():
+        met = greet([ring("rows", 1), ring("rows", -1)] + others())
+        each(begin, pieces, lambda c: start(loads(c)))
+        met()
+        each(leave, pieces, lambda c: start(y_copies(c)))
+
+        def piece(c, landed):
+            for k in range(L):
+                i = c * L + k
+                r = (c - begin) * L + k
+                for p, y in enumerate((0, ny - 1)):
+                    below = halo[0, (c - leave) * L + k] if landed and p == 0 else even[y, i + 1]
+                    above = halo[1, (c - leave) * L + k] if landed and p == 1 else even[y + 2, i + 1]
+                    value = next_value(
+                        even[y + 1, i + 1], below, above, even[y + 1, i], even[y + 1, i + 2],
+                        z_end[0, y, pl.ds(i, 1)], z_end[1, y, pl.ds(i, 1)], mob[p, r], src[p, r],
+                    )
+                    rest[p, r] = value
+                    line_stats(stats, value, c - begin, 2 * k + p)
+            start(my_stats(c))
+
+        def held(c):
+            wait(loads(c))
+            piece(c, False)
+
+        def moved(c):
+            wait(loads(c))
+            arrived(y_copies(c))
+            piece(c, True)
+
+        each(begin, leave, held)
+        each(leave, pieces, moved)
+        each(leave, pieces, lambda c: sent(y_copies(c)))
+
+        def drain(c):
+            sent(my_stats(c))
+            arrived(my_stats(c))
+
+        each(begin, pieces, drain)
+
+
+def write_planes(first, end, planes, stats, value_of, block_of, at, anomaly, field_end, held, sems):
+    _, _, nz, _ = field_end.shape
+    slabs = stats.shape[0]
+
+    def field_copies(c):
         lines = pl.ds(c * L, L)
-        return pltpu.make_async_copy(held.at[:, lines], anomaly.at[:, lines], sems.at[1, c])
+        return [pltpu.make_async_copy(block_of(c, p), field_end.at[y, lines], sems.at[0, y, c]) for p, y in enumerate(planes)]
+
+    def anomaly_copies(c):
+        lines = pl.ds(c * L, L)
+        return [pltpu.make_async_copy(held.at[y, lines], anomaly.at[y, lines], sems.at[1, y, c]) for y in planes]
 
     def piece(c):
-        stats = stats_of(c)
-        slabs = len(stats)
-        mean = sum((a for a, _ in stats[1:]), stats[0][0]) * (1.0 / slabs)
-        spread = sum((b for _, b in stats[1:]), stats[0][1])
-        for a, _ in stats:
-            spread = spread + (a - mean) * (a - mean) * float(nz)
+        means = [stats[d, c - at, 0] for d in range(slabs)]
+        mean = sum(means[1:], means[0]) * (1.0 / slabs)
+        spread = stats[0, c - at, 1]
+        for d in range(1, slabs):
+            spread = spread + stats[d, c - at, 1]
+        for other in means:
+            spread = spread + (other - mean) * (other - mean) * float(nz)
         scale = lax.rsqrt(spread * (1.0 / (nz * slabs)) + EPS)
         for k in range(L):
-            for y in range(ny):
-                r = k * ny + y
-                held[y, c * L + k] = (value_of(c, k, y) - mean[r:r + 1]) * scale[r:r + 1]
-        anomaly_copy(c).start()
-
-    each(first, end, lambda c: field_copy(c).start())
-    each(first, end, piece)
+            for p, y in enumerate(planes):
+                r = 2 * k + p
+                held[y, c * L + k] = (value_of(c, k, p) - mean[r:r + 1]) * scale[r:r + 1]
+        start(anomaly_copies(c))
 
     def done(c):
-        field_copy(c).wait()
-        anomaly_copy(c).wait()
-
-    each(first, end, done)
-
-
-def first_write(odd, stats, anomaly, field_end, after, held, sems):
-    ny = field_end.shape[0]
-    slabs = stats.shape[0]
-    write_pieces(
-        0, leaving() - HOLD,
-        lambda c: [(stats[d, c, 0], stats[d, c, 1]) for d in range(slabs)],
-        lambda c, k, y: odd[y + 1, c * L + k + 1],
-        lambda c: odd.at[pl.ds(1, ny), pl.ds(c * L + 1, L)],
-        anomaly, field_end, held, sems,
+        wait(field_copies(c))
+        wait(anomaly_copies(c))
+
+    return (
+        lambda: each(first, end, lambda c: start(field_copies(c))),
+        lambda: each(first, end, piece),
+        lambda: each(first, end, done),
     )
+
+
+def first_write(odd, inner_stats, outer_stats, anomaly, field_end, after, held, sems):
+    ny, nx = field_end.shape[:2]
+
+    def from_odd(first, end, planes, stats):
+        return write_planes(
+            first, end, planes, stats,
+            lambda c, k, p: odd[planes[p] + 1, c * L + k + 1],
+            lambda c, p: odd.at[planes[p] + 1, pl.ds(c * L + 1, L)],
+            0, anomaly, field_end, held, sems,
+        )
+
+    parts = (from_odd(0, nx // L, INNER, inner_stats), from_odd(0, beginning(), (0, ny - 1), outer_stats))
+    for phase in zip(*parts):
+        for run in phase:
+            run()
     after[...] = jnp.zeros_like(after)
 
 
 def second_write(rest, stats, _a, _f, anomaly, field_end, held, sems):
-    slabs = stats.shape[0]
-    begin = leaving() - HOLD
-    write_pieces(
-        begin, field_end.shape[1] // L,
-        lambda c: [(stats[d, c - begin, 0], stats[d, c - begin, 1]) for d in range(slabs)],
-        lambda c, k, y: rest[y, (c - begin) * L + k],
-        lambda c: rest.at[:, pl.ds((c - begin) * L, L)],
-        anomaly, field_end, held, sems,
-    )
+    ny, nx = field_end.shape[:2]
+    begin = beginning()
+    for run in write_planes(
+        begin, nx // L, (0, ny - 1), stats,
+        lambda c, k, p: rest[p, (c - begin) * L + k],
+        lambda c, p: rest.at[p, pl.ds((c - begin) * L, L)],
+        begin, anomaly, field_end, held, sems,
+    ):
+        run()
 
 
 def near(x):
@@ -410,18 +435,19 @@
     vmem = pl.BlockSpec(memory_space=pltpu.VMEM)
     padded = (ny + 2, nx + 2, nz, levels)
     faces = (2, ny, nx, levels)
-    left = pieces - min(LEAVE) + HOLD
+    left = pieces - min(leave - hold for leave, hold in zip(LEAVE, HOLD))
     coming = pieces - min(LEAVE)
-    odd, even, z_end, stats = pl.pallas_call(
+    odd, even, z_end, inner_stats, outer_stats = pl.pallas_call(
         first_kernel,
         out_shape=(
             pltpu.VMEM(padded, f32),
             pltpu.VMEM(padded, f32),
             pltpu.VMEM(faces, f32),
-            pltpu.VMEM((slabs, pieces, 2, L * ny, levels), f32),
+            pltpu.VMEM((slabs, pieces, 2, L * 2, levels), f32),
+            pltpu.VMEM((slabs, pieces, 2, L * 2, levels), f32),
         ),
         in_specs=[any_space] * 3,
-        out_specs=(vmem,) * 4,
+        out_specs=(vmem,) * 5,
         scratch_shapes=[
             pltpu.VMEM(field.shape, f32),
             pltpu.VMEM(field.shape, f32),
@@ -433,6 +459,8 @@
             DMA((STEPS, 2)),
             DMA((STEPS, 2)),
             DMA((STEPS, 2)),
+            DMA((slabs - 1,)),
+            DMA((slabs - 1,)),
             DMA((slabs - 1, pieces)),
             DMA((slabs - 1, pieces)),
             DMA((7,)),
@@ -444,34 +472,34 @@
     )(field, mobility, source)
     shape = jax.ShapeDtypeStruct(field.shape, f32)
     writing = dict(
-        scratch_shapes=[pltpu.VMEM(field.shape, f32), DMA((2, pieces))],
+        scratch_shapes=[pltpu.VMEM(field.shape, f32), DMA((2, ny, pieces))],
         compiler_params=pltpu.CompilerParams(vmem_limit_bytes=12 * 2**20),
     )
     anomaly, field_end, after = pl.pallas_call(
         first_write,
         out_shape=(shape, shape, jax.ShapeDtypeStruct((8, levels), f32)),
-        in_specs=[vmem, vmem],
+        in_specs=[vmem, vmem, vmem],
         out_specs=(any_space, any_space, vmem),
         name="write",
         **writing,
-    )(near(odd), near(stats))
+    )(near(odd), near(inner_stats), near(outer_stats))
     rest, stats = pl.pallas_call(
         second_kernel,
         out_shape=(
-            pltpu.VMEM((ny, left * L, nz, levels), f32),
-            pltpu.VMEM((slabs, left, 2, L * ny, levels), f32),
+            pltpu.VMEM((2, left * L, nz, levels), f32),
+            pltpu.VMEM((slabs, left, 2, L * 2, levels), f32),
         ),
         in_specs=[vmem, vmem, any_space, any_space, any_space],
         out_specs=(vmem, vmem),
         scratch_shapes=[
-            pltpu.VMEM((ny, left * L, nz, levels), f32),
-            pltpu.VMEM((ny, left * L, nz, levels), f32),
+            pltpu.VMEM((2, left * L, nz, levels), f32),
+            pltpu.VMEM((2, left * L, nz, levels), f32),
             pltpu.VMEM((2, coming * L, nz, levels), f32),
             DMA((2, coming)),
             DMA((2, coming)),
             DMA((slabs - 1, left)),
             DMA((slabs - 1, left)),
-            DMA((2, left)),
+            DMA((2, 2, left)),
         ],
         name="rest",
         compiler_params=pltpu.CompilerParams(

time: 152 us -> 149 us (0.980)
  Pallas kernels: 151 us -> 149 us
    pallas_call x1, Pallas kernels: 131 us -> 128 us  [per_device(): pl.pallas_call(first_kernel, out_shape=(pltpu.VMEM(padded, f32), pltpu.VM...]
where the time goes in v3:
time: 149 us
  Pallas kernels  149 us (100%)
    pallas_call x1, Pallas kernels, per_device(): pl.pallas_call(first_kernel, out_shape=(pltpu.VMEM(padded, f32), pltpu.VM...  128 us
    pallas_call x1, Pallas kernels, per_device(): pl.pallas_call(second_kernel, out_shape=(pltpu.VMEM((2, left * L, nz, lev...  13.1 us
    pallas_call x1, Pallas kernels, per_device(): pl.pallas_call(first_write, out_shape=(shape, shape, jax.ShapeDtypeStruct...  5.72 us

profile of v3, /device:TPU:0, one launch (start us, length us, event | category | flops | bytes accessed | tf_op | source)
XLA Modules:
  0.0 149.4 jit_solution(14512748487577832469)
XLA Ops:
  0.6 128.0 %steps.1 = (f32[6,34,128,128]{3,2,1,0:T(8,128)S(1)}, f32[6,34,128,128]{3,2,1,0:T(8,128)S(1)}, f32[2,4,32,128]{3,2,1,0:T(8,128)S(1)}, f32[4,8,2,8,128]{4,3,2,1,0:T(8,128)S(1)}, f32[4,8,2,8,128]{4,3,2,1,0:T(8,128)S(1)}) custom-call(f32[4,32,128,128]{3,2,1,0:T(8,128)} %field.1, f32[4,32,128,128]{3,2,1,0:T(8,128)} %mobility.3, f32[4,32,128,128]{3,2,1,0:T(8,128)} %source.3), custom_call_target="tpu_custom_call" | custom-call | tf_op jit(solution)/shard_map/steps/pallas_call | solution.py:440
  128.7 5.7 %write.1 = (f32[4,32,128,128]{3,2,1,0:T(8,128)}, f32[4,32,128,128]{3,2,1,0:T(8,128)}, f32[8,128]{1,0:T(8,128)S(1)}) custom-call(f32[6,34,128,128]{3,2,1,0:T(8,128)S(1)} %get-tuple-element.14.odd, f32[4,8,2,8,128]{4,3,2,1,0:T(8,128)S(1)} %get-tuple-element.15.inner_stats, f32[4,8,2,8,128]{4,3,2,1,0:T(8,128)S(1)} %get-tuple-element.16.outer_stats), custom_call_target="tpu_custom_call" | custom-call | tf_op jit(solution)/shard_map/write/pallas_call | solution.py:478
  134.4 13.1 %rest.1 = (f32[2,24,128,128]{3,2,1,0:T(8,128)S(1)}, f32[4,6,2,8,128]{4,3,2,1,0:T(8,128)S(1)}) custom-call(f32[6,34,128,128]{3,2,1,0:T(8,128)S(1)} %get-tuple-element.12.even, f32[2,4,32,128]{3,2,1,0:T(8,128)S(1)} %get-tuple-element.13.z_end, f32[4,32,128,128]{3,2,1,0:T(8,128)} %mobility.3, f32[4,32,128,128]{3,2,1,0:T(8,128)} %source.3, ...), custom_call_target="tpu_custom_call" | custom-call | tf_op jit(solution)/shard_map/rest/pallas_call | solution.py:486
  147.5 1.9 %write_rest.1 = (f32[4,32,128,128]{3,2,1,0:T(8,128)}, f32[4,32,128,128]{3,2,1,0:T(8,128)}) custom-call(f32[2,24,128,128]{3,2,1,0:T(8,128)S(1)} %get-tuple-element.18.rest, f32[4,6,2,8,128]{4,3,2,1,0:T(8,128)S(1)} %get-tuple-element.19.stats, f32[4,32,128,128]{3,2,1,0:T(8,128)} %get-tuple-element.20._a, ...), custom_call_target="tpu_custom_call", output_to_operand_aliasing={{0}: (2, {}), {1}: (3, {})} | custom-call | tf_op jit(solution)/shard_map/write_rest/pallas_call | solution.py:509

commit v4 on v3

--- a/solution.py
+++ b/solution.py
@@ -6,7 +6,7 @@
 from jax.sharding import PartitionSpec as P
 
 STEPS = 3
-LINES = (4, 4, 4)
+LINES = (8, 8, 4)
 L = LINES[-1]
 LEAVE = (7, 3)
 HOLD = (1, 1)

time: 149 us -> 149 us (level)
  no operation moved by 1% of the time
where the time goes in v4:
time: 149 us
  Pallas kernels  149 us (100%)
    pallas_call x1, Pallas kernels, per_device(): pl.pallas_call(first_kernel, out_shape=(pltpu.VMEM(padded, f32), pltpu.VM...  128 us
    pallas_call x1, Pallas kernels, per_device(): pl.pallas_call(second_kernel, out_shape=(pltpu.VMEM((2, left * L, nz, lev...  13 us
    pallas_call x1, Pallas kernels, per_device(): pl.pallas_call(first_write, out_shape=(shape, shape, jax.ShapeDtypeStruct...  5.72 us

profile of v4, /device:TPU:0, one launch (start us, length us, event | category | flops | bytes accessed | tf_op | source)
XLA Modules:
  0.0 149.3 jit_solution(11171880480922128032)
XLA Ops:
  0.6 128.0 %steps.1 = (f32[6,34,128,128]{3,2,1,0:T(8,128)S(1)}, f32[6,34,128,128]{3,2,1,0:T(8,128)S(1)}, f32[2,4,32,128]{3,2,1,0:T(8,128)S(1)}, f32[4,8,2,8,128]{4,3,2,1,0:T(8,128)S(1)}, f32[4,8,2,8,128]{4,3,2,1,0:T(8,128)S(1)}) custom-call(f32[4,32,128,128]{3,2,1,0:T(8,128)} %field.1, f32[4,32,128,128]{3,2,1,0:T(8,128)} %mobility.3, f32[4,32,128,128]{3,2,1,0:T(8,128)} %source.3), custom_call_target="tpu_custom_call" | custom-call | tf_op jit(solution)/shard_map/steps/pallas_call | solution.py:440
  128.6 5.7 %write.1 = (f32[4,32,128,128]{3,2,1,0:T(8,128)}, f32[4,32,128,128]{3,2,1,0:T(8,128)}, f32[8,128]{1,0:T(8,128)S(1)}) custom-call(f32[6,34,128,128]{3,2,1,0:T(8,128)S(1)} %get-tuple-element.14.odd, f32[4,8,2,8,128]{4,3,2,1,0:T(8,128)S(1)} %get-tuple-element.15.inner_stats, f32[4,8,2,8,128]{4,3,2,1,0:T(8,128)S(1)} %get-tuple-element.16.outer_stats), custom_call_target="tpu_custom_call" | custom-call | tf_op jit(solution)/shard_map/write/pallas_call | solution.py:478
  134.4 13.0 %rest.1 = (f32[2,24,128,128]{3,2,1,0:T(8,128)S(1)}, f32[4,6,2,8,128]{4,3,2,1,0:T(8,128)S(1)}) custom-call(f32[6,34,128,128]{3,2,1,0:T(8,128)S(1)} %get-tuple-element.12.even, f32[2,4,32,128]{3,2,1,0:T(8,128)S(1)} %get-tuple-element.13.z_end, f32[4,32,128,128]{3,2,1,0:T(8,128)} %mobility.3, f32[4,32,128,128]{3,2,1,0:T(8,128)} %source.3, ...), custom_call_target="tpu_custom_call" | custom-call | tf_op jit(solution)/shard_map/rest/pallas_call | solution.py:486
  147.4 1.9 %write_rest.1 = (f32[4,32,128,128]{3,2,1,0:T(8,128)}, f32[4,32,128,128]{3,2,1,0:T(8,128)}) custom-call(f32[2,24,128,128]{3,2,1,0:T(8,128)S(1)} %get-tuple-element.18.rest, f32[4,6,2,8,128]{4,3,2,1,0:T(8,128)S(1)} %get-tuple-element.19.stats, f32[4,32,128,128]{3,2,1,0:T(8,128)} %get-tuple-element.20._a, ...), custom_call_target="tpu_custom_call", output_to_operand_aliasing={{0}: (2, {}), {1}: (3, {})} | custom-call | tf_op jit(solution)/shard_map/write_rest/pallas_call | solution.py:509
